TPU v7x, 32 devices: a whole 2x2x4 slice. The times are simulated.
32 devices in a mesh: row: 8 (over y, x, core), col: 4 (over z).
Axes of the slice: x: 2, y: 2, z: 4, core: 2. Of those that a mesh axis runs over, the one named last changes fastest.
Arguments:
- tangents: float32 [192, 128, 6144], P('row', None, 'col'), may hold values from -6 to 6
- base_flow: float32 [192, 128, 192], P('row', None, 'col'), may hold values from -0.0625 to 0.0625
- mode_mask: int32 [192, 192], P('row', 'col'), may hold values 0 or 1
- decay_rates: float32 [128], replicated, may hold values from 1 to 100
- to_eigen: float32 [128, 128], replicated, may hold values from -0.5 to 0.5
- from_eigen: float32 [128, 128], replicated, may hold values from -0.5 to 0.5
Outputs:
- vectors: float32 [192, 128, 6144], P('row', None, 'col')
- growth: float32 [32], replicated
Inputs may be any that keep to these rules, and one draw needn't show every extreme that they name: `mode_mask`: 1 keeps a mode pair of the linearized product, 0 removes it.
All inputs are finite; a program needn't handle non-finite values. No bound on the sum of `mode_mask` on one device may be relied on, other than what follows from the above.
Results may differ from a plain program's by a relative error of at most 0.00005.
Values sent between devices are 32-bit elements; how exact they have to be, the bound alone decides.
A program may use at most 256 MiB of HBM per device.

v0:
```python
import math

import jax
import jax.numpy as jnp
from jax import lax
from jax.sharding import PartitionSpec as P

PRECISE = lax.Precision.HIGHEST
STEP_COEF = 10.0
VISCOSITY = 0.01
ALPHA_X = 0.5
BETA_Z = 1.0


def local_waves(points_count, first_index, length):
    indices = first_index + jnp.arange(length, dtype=jnp.int32)
    middle = points_count // 2
    return jnp.where(indices <= middle, indices, indices - middle).astype(jnp.float32)


def synthesis(points_count):
    points = jnp.arange(points_count, dtype=jnp.int32)[:, None]
    mode_index = jnp.arange(points_count, dtype=jnp.int32)[None, :]
    middle = points_count // 2
    wave_index = jnp.where(mode_index <= middle, mode_index, mode_index - middle)
    turn_count = (points * wave_index % points_count).astype(jnp.float32)
    angles = turn_count * (2.0 * math.pi / points_count)
    return jnp.where(mode_index <= middle, jnp.cos(angles), jnp.sin(angles))


def analysis(points_count):
    mode_index = jnp.arange(points_count, dtype=jnp.int32)
    middle = points_count // 2
    weights = jnp.where(
        (mode_index == 0) | (mode_index == middle),
        jnp.float32(1.0 / points_count),
        jnp.float32(2.0 / points_count),
    )
    return weights[:, None] * synthesis(points_count).T


def derivative_analysis(points_count, wave_scale):
    rows_index = jnp.arange(points_count, dtype=jnp.int32)[:, None]
    cols_index = jnp.arange(points_count, dtype=jnp.int32)[None, :]
    middle = points_count // 2
    rising = (cols_index == rows_index + middle) & (rows_index >= 1) & (rows_index < middle)
    falling = (rows_index == cols_index + middle) & (cols_index >= 1) & (cols_index < middle)
    rows_float = jnp.broadcast_to(rows_index.astype(jnp.float32), (points_count, points_count))
    cols_float = jnp.broadcast_to(cols_index.astype(jnp.float32), (points_count, points_count))
    derivative = jnp.where(rising, rows_float, jnp.float32(0.0)) - jnp.where(
        falling, cols_float, jnp.float32(0.0)
    )
    return -wave_scale * jnp.dot(derivative, analysis(points_count), precision=PRECISE)


def denominators(decay_rates, x_count, z_count, x_start, z_start, x_length, z_length):
    wave_x = ALPHA_X * local_waves(x_count, x_start, x_length)
    wave_z = BETA_Z * local_waves(z_count, z_start, z_length)
    return (
        STEP_COEF
        + VISCOSITY * (wave_x[:, None, None] ** 2 + wave_z[None, None, :] ** 2)
        + decay_rates[None, :, None]
    )


def body(tangents, base_flow, mode_mask, decay_rates, to_eigen, from_eigen):
    x_length, y_count, zv_length = tangents.shape
    z_length = base_flow.shape[2]
    vec_count = zv_length // z_length
    row_devices = lax.axis_size("row")
    col_devices = lax.axis_size("col")
    x_count = x_length * row_devices
    z_count = z_length * col_devices
    x_synthesis = synthesis(x_count)
    z_synthesis = synthesis(z_count)
    x_derivative = derivative_analysis(x_count, ALPHA_X)
    z_analysis = analysis(z_count)
    all_devices = row_devices * col_devices
    plane_count = y_count // all_devices
    stacked = tangents.reshape(x_length, y_count, 1, zv_length)
    speed_stack = base_flow.reshape(x_length, y_count, 1, z_length)
    planes, speed_field = (
        lax.all_to_all(stacked, ("row", "col"), split_axis=1, concat_axis=2, tiled=True),
        lax.all_to_all(speed_stack, ("row", "col"), split_axis=1, concat_axis=2, tiled=True),
    )
    x_table = x_synthesis.reshape(x_count, row_devices, x_length)
    z_table = z_synthesis.reshape(z_count, col_devices, z_length)
    planes = planes.reshape(x_length, plane_count, row_devices, col_devices, z_length, vec_count)
    physical = jnp.einsum("myrcnv,prm->ypcnv", planes, x_table, precision=PRECISE)
    physical = jnp.einsum("ypcnv,scn->ypsv", physical, z_table, precision=PRECISE)
    speed_field = speed_field.reshape(x_length, plane_count, row_devices, col_devices, z_length)
    speed_field = jnp.einsum("myrcn,prm->ypcn", speed_field, x_table, precision=PRECISE)
    speed_field = jnp.einsum("ypcn,scn->yps", speed_field, z_table, precision=PRECISE)
    product = physical * speed_field[:, :, :, None]
    returned = jnp.einsum("ypsv,ns->ypnv", product, z_analysis, precision=PRECISE)
    returned = jnp.einsum("ypnv,mp->ymnv", returned, x_derivative, precision=PRECISE)
    returned = returned.reshape(
        plane_count, row_devices, x_length, col_devices, z_length, vec_count
    )
    returned = jnp.transpose(returned, (2, 0, 1, 3, 4, 5)).reshape(
        x_length, plane_count, all_devices, zv_length
    )
    nonlinear = lax.all_to_all(returned, ("row", "col"), split_axis=2, concat_axis=1, tiled=True)
    nonlinear = nonlinear.reshape(x_length, y_count, zv_length)
    x_start = lax.axis_index("row") * x_length
    z_start = lax.axis_index("col") * z_length
    divisor = denominators(decay_rates, x_count, z_count, x_start, z_start, x_length, z_length)
    retained = mode_mask.astype(jnp.float32)[:, None, :, None]
    nonlinear = nonlinear.reshape(x_length, y_count, z_length, vec_count) * retained
    right_side = STEP_COEF * tangents.reshape(x_length, y_count, z_length, vec_count) + nonlinear
    eigen_part = jnp.einsum(
        "ji,mic->mjc", to_eigen, right_side.reshape(x_length, y_count, zv_length), precision=PRECISE
    )
    eigen_part = eigen_part.reshape(x_length, y_count, z_length, vec_count) / divisor[:, :, :, None]
    stepped = jnp.einsum(
        "yj,mjc->myc",
        from_eigen,
        eigen_part.reshape(x_length, y_count, zv_length),
        precision=PRECISE,
    )
    columns = stepped.reshape(x_length * y_count * z_length, vec_count)
    cell_count = x_count * y_count * z_count
    identity = jnp.eye(vec_count, dtype=jnp.float32)

    def refine(block):
        local_gram = jnp.einsum("cv,cu->vu", block, block, precision=PRECISE)
        gram_matrix = lax.psum(local_gram, ("row", "col")) / cell_count
        lower_factor = jnp.linalg.cholesky(gram_matrix)
        inverse = jax.scipy.linalg.solve_triangular(lower_factor, identity, lower=True)
        refined = jnp.einsum("cv,uv->cu", block, inverse, precision=PRECISE)
        return (refined, jnp.log(jnp.diagonal(lower_factor)))

    first_pass, first_growth = refine(columns)
    orthonormal, second_growth = refine(first_pass)
    growth = first_growth + second_growth
    return (orthonormal.reshape(x_length, y_count, zv_length), growth)


def solution(mesh):
    placed = (P("row", None, "col"), P("row", None, "col"), P("row", "col"), P(), P(), P())
    return jax.shard_map(
        body, mesh=mesh, in_specs=placed, out_specs=(P("row", None, "col"), P()), check_vma=False
    )
```

profile of v0, /device:TPU:0, one launch (start us, length us, event | category | flops | bytes accessed | tf_op | source)
XLA Modules:
  0.0 2041.6 jit_solution(13407496623339631732)
XLA Ops:
  0.6 1.6 copy.62
  2.4 2.4 reshape.235
  4.8 7.3 all-to-all-start.1
  12.1 19.6 copy.107
  31.7 6.1 all-to-all-start
  38.0 1.3 fusion.19
  39.3 0.9 fusion.148
  40.7 2.0 reduce.4
  42.7 0.7 reshape.236
  43.4 3.4 fusion.16
  46.8 1.7 convolution_bitcast_fusion.1
  48.5 394.0 %all-to-all-done = f32[24,128,1,1536]{3,0,2,1:T(8,128)} async-done(((f32[24,128,1,1536]{3,0,2,1:T(8,128)}), f32[24,128,1,1536]{3,0,2,1:T(8,128)}, u32[]{:S(2)}, u32[]{:S(2)}) %all-to-all-start) | async-done | bytes 18874400 | tf_op jit(solution)/shard_map/all_to_all | solution.py:83
  442.5 19.6 copy.106
  462.2 44.8 %reshape.204 = f32[24,4,8,4,48,32]{5,4,3,2,1,0:T(8,128)} reshape(f32[24,4,32,1,1536]{4,2,1,0,3:T(8,128)} %bitcast.144) | data formatting | bytes 37748736 | tf_op jit(solution)/shard_map/reshape | solution.py:88
  507.0 67.4 %copy.60 = f32[24,4,8,4,48,32]{4,0,2,5,3,1:T(8,128)} copy(f32[24,4,8,4,48,32]{5,4,3,2,1,0:T(8,128)} %reshape.204) | data formatting | bytes 37748736 | tf_op jit(solution)/shard_map/reshape | solution.py:88
  574.4 86.3 %fusion.28 = f32[192,4,4,48,32,1]{0,3,5,4,2,1:T(8,128)} fusion(f32[24,4,8,4,48,32]{4,0,2,5,3,1:T(8,128)} %copy.60, f32[192,8,24,1,1,1]{0,2,1,5,4,3:T(8,128)S(1)} %fusion.148), kind=kOutput, calls=%fused_computation.36 | convolution fusion | flops 10871635968 | bytes 37896192 | tf_op jit(solution)/shard_map/myrcnv,prm->ypcnv/dot_general | solution.py:89
  660.7 31.7 %fusion.1 = f32[192,4,192,32,1]{2,0,3,4,1:T(8,128)} fusion(f32[192,4,4,48,32,1]{0,3,5,4,2,1:T(8,128)} %fusion.28, s32[4,48]{1,0:T(4,128)S(1)} %add_select_fusion.4, pred[4,48]{1,0:T(4,128)(4,1)S(1)} %fusion.103), kind=kOutput, calls=%fused_computation.4 | convolution fusion | flops 10872004608 | bytes 37749696 | tf_op jit(solution)/shard_map/ypcnv,scn->ypsv/dot_general | solution.py:90
  692.4 30.9 %fusion = f32[192,4,192,32]{2,0,3,1:T(8,128)} fusion(f32[192,4,192,32,1]{2,0,3,4,1:T(8,128)} %fusion.1, f32[4,192,192]{1,2,0:T(8,128)S(1)} %convolution_bitcast_fusion.1, s32[192]{0:T(256)S(1)} %get-tuple-element.8, f32[192]{0:T(256)S(1)} %or_select_fusion, pred[192]{0:T(512)(128)(4,1)S(1)} %get-tuple-element.10), kind=kOutput, calls=%fused_computation.3 | convolution fusion | flops 10876760064 | bytes 38340288 | tf_op jit(solution)/shard_map/ypsv,ns->ypnv/dot_general | solution.py:95
  723.3 28.1 %fusion.9 = f32[4,192,192,32]{2,1,3,0:T(8,128)} fusion(f32[192,192,1,1]{1,0,3,2:T(8,128)S(1)} %fusion.19, f32[192,4,192,32]{2,0,3,1:T(8,128)} %fusion), kind=kOutput, calls=%fused_computation.16 | convolution fusion | flops 10871635968 | bytes 37896192 | tf_op jit(solution)/shard_map/ypnv,mp->ymnv/dot_general | solution.py:96
  751.4 44.9 %reshape.207 = f32[4,8,24,4,48,32]{4,3,2,1,5,0:T(4,128)} reshape(f32[4,192,192,32]{2,1,3,0:T(8,128)} %fusion.9) | data formatting | bytes 37748736 | tf_op jit(solution)/shard_map/reshape | solution.py:97
  796.3 71.3 %copy.68 = f32[4,8,24,4,48,32]{5,4,3,1,0,2:T(8,128)} copy(f32[4,8,24,4,48,32]{4,3,2,1,5,0:T(4,128)} %reshape.207) | data formatting | bytes 37748736 | tf_op jit(solution)/shard_map/reshape | solution.py:97
  867.7 53.6 %reshape.208 = f32[24,4,32,1536]{3,2,1,0:T(8,128)} reshape(f32[24,4,8,4,48,32]{5,4,3,2,1,0:T(8,128)} %bitcast.33) | data formatting | bytes 37748736 | tf_op jit(solution)/shard_map/reshape | solution.py:100
  921.3 23.2 %copy.69 = f32[24,4,32,1536]{3,1,0,2:T(4,128)} copy(f32[24,4,32,1536]{3,2,1,0:T(8,128)} %reshape.208) | data formatting | bytes 37748736 | tf_op jit(solution)/shard_map/reshape | solution.py:100
  944.5 17.9 all-to-all-start.2
  963.8 403.4 %all-to-all-done.2 = f32[24,4,32,1536]{3,1,0,2:T(4,128)} async-done(((f32[24,4,32,1536]{3,1,0,2:T(4,128)}), f32[24,4,32,1536]{3,1,0,2:T(4,128)}, u32[]{:S(2)}, u32[]{:S(2)}) %all-to-all-start.2) | async-done | bytes 18874400 | tf_op jit(solution)/shard_map/all_to_all | solution.py:103
  1367.1 12.1 copy.70
  1379.2 20.4 %fusion.5 = f32[24,128,1536]{2,0,1:T(8,128)} fusion(f32[24,4,32,1536]{3,0,1,2:T(8,128)S(1)} %copy.70, f32[24,128,1536]{2,1,0:T(8,128)} %param.9, f32[24,1536]{1,0:T(8,128)S(1)} %mul.166), kind=kLoop, calls=%fused_computation.9 | loop fusion | flops 14155776 | bytes 56770560 | tf_op jit(solution)/shard_map/add | solution.py:110
  1399.7 38.5 %bitcast_divide_fusion = f32[24,128,1536]{1,2,0:T(8,128)S(1)} fusion(f32[24,128,48]{1,2,0:T(8,128)S(1)} %broadcast_add_fusion, f32[24,128,1536]{2,0,1:T(8,128)} %fusion.5, f32[128,128]{1,0:T(8,128)S(1)} %copy-done), kind=kOutput, calls=%fused_computation.10 | convolution fusion | flops 7252475904 | bytes 38404096 | tf_op jit(solution)/shard_map/ji,mic->mjc/dot_general | solution.py:111
  1438.2 17.9 convolution_bitcast_fusion
  1456.1 18.7 copy.72
  1474.8 44.8 %reshape.209 = f32[147456,32]{1,0:T(8,128)} reshape(f32[24,128,1536]{2,1,0:T(8,128)} %copy.72) | data formatting | bytes 37748736 | tf_op jit(solution)/shard_map/reshape | solution.py:121
  1519.6 129.6 %fusion.129 = f32[32,32]{0,1:T(8,128)S(1)} fusion(f32[147456,32]{1,0:T(8,128)} %reshape.209), kind=kOutput, calls=%fused_computation.172 | convolution fusion | flops 1811939328 | bytes 18878464 | tf_op jit(solution)/shard_map/cv,cu->vu/dot_general | solution.py:126
  1649.2 53.2 %psum.14 = f32[32,32]{0,1:T(8,128)S(1)} all-reduce(f32[32,32]{0,1:T(8,128)S(1)} %fusion.129), channel_id=1, replica_groups=mesh['row'=8,'col'=4] {'row','col'}, use_global_device_ids=true, to_apply=%region_0.1 | all-reduce | flops 1024 | bytes 8192 | tf_op jit(solution)/shard_map/psum | solution.py:127
  1702.5 2.9 cholesky.44
  1705.5 0.6 compare_reduce_fusion.1
  1706.1 0.7 select_bitcast_fusion.1
  1706.8 2.4 custom-call.10
  1709.4 85.6 %fusion.130 = f32[147456,32]{0,1:T(8,128)} fusion(f32[147456,32]{1,0:T(8,128)} %reshape.209, f32[32,32]{1,0:T(8,128)S(1)} %fusion.95), kind=kOutput, calls=%fused_computation.173 | convolution fusion | flops 1811939328 | bytes 37752832 | tf_op jit(solution)/shard_map/cv,uv->cu/dot_general | solution.py:130
  1795.0 19.3 fusion.131
  1814.4 39.5 %psum.15 = f32[32,32]{0,1:T(8,128)S(1)} all-reduce(f32[32,32]{0,1:T(8,128)S(1)} %fusion.131), channel_id=1, replica_groups=mesh['row'=8,'col'=4] {'row','col'}, use_global_device_ids=true, to_apply=%region_3.6 | all-reduce | flops 1024 | bytes 8192 | tf_op jit(solution)/shard_map/psum | solution.py:127
  1854.0 2.9 cholesky.55
  1856.9 0.6 compare_reduce_fusion
  1857.6 0.7 select_bitcast_fusion
  1858.2 0.7 gather_fusion.1
  1859.0 0.7 gather_fusion
  1859.7 2.4 custom-call.11
  1862.3 124.7 %fusion.132 = f32[147456,32]{1,0:T(8,128)} fusion(f32[147456,32]{0,1:T(8,128)} %fusion.130, f32[32,32]{1,0:T(8,128)S(1)} %fusion.93), kind=kOutput, calls=%fused_computation.175 | convolution fusion | flops 1811939328 | bytes 37752832 | tf_op jit(solution)/shard_map/cv,uv->cu/dot_general | solution.py:130
  1987.1 53.6 %reshape.210 = f32[24,128,1536]{2,1,0:T(8,128)} reshape(f32[147456,32]{1,0:T(8,128)} %fusion.132) | data formatting | bytes 37748736 | tf_op jit(solution)/shard_map/reshape | solution.py:136
  (43 shorter events, 3.2 us)
Async XLA Ops:
  0.6 1399.0 %copy-start = (f32[128,128]{1,0:T(8,128)S(1)}, f32[128,128]{1,0:T(8,128)}, u32[]{:S(2)}) copy-start(f32[128,128]{1,0:T(8,128)} %param.13) | copy-start | bytes 196612
  4.8 27.0 %all-to-all-start.1 = ((f32[32,1,4608]{2,1,0:T(1,128)}), f32[32,1,4608]{2,1,0:T(1,128)S(1)}, u32[]{:S(2)}, u32[]{:S(2)}) async-start(f32[32,1,4608]{2,1,0:T(1,128)} %reshape.235), calls=%async_computation.1 | async-start | bytes 1179648 | tf_op jit(solution)/shard_map/all_to_all | solution.py:84
  31.7 410.8 %all-to-all-start = ((f32[24,128,1,1536]{3,0,2,1:T(8,128)}), f32[24,128,1,1536]{3,0,2,1:T(8,128)}, u32[]{:S(2)}, u32[]{:S(2)}) async-start(f32[24,128,1,1536]{3,0,2,1:T(8,128)} %bitcast.143), calls=%async_computation | async-start | bytes 37748736 | tf_op jit(solution)/shard_map/all_to_all | solution.py:83
  944.5 17.9 copy-start.4
  944.5 19.0 copy-start.5
  944.5 422.6 %all-to-all-start.2 = ((f32[24,4,32,1536]{3,1,0,2:T(4,128)}), f32[24,4,32,1536]{3,1,0,2:T(4,128)}, u32[]{:S(2)}, u32[]{:S(2)}) async-start(f32[24,4,32,1536]{3,1,0,2:T(4,128)} %copy.69), calls=%async_computation.2 | async-start | bytes 37748736 | tf_op jit(solution)/shard_map/all_to_all | solution.py:103
  1399.7 38.5 %copy-start.3 = (f32[128,128]{1,0:T(8,128)S(1)}, f32[128,128]{1,0:T(8,128)}, u32[]{:S(2)}) copy-start(f32[128,128]{1,0:T(8,128)} %param.14) | copy-start | bytes 196612
  1795.0 63.2 %copy-start.2 = (s32[32]{0:T(128)S(1)}, s32[32]{0:T(128)}, u32[]{:S(2)}) copy-start(s32[32]{0:T(128)} %or_bitcast_fusion) | copy-start | bytes 388
  1987.1 54.1 %copy-start.1 = (f32[128,128]{1,0:T(8,128)S(1)}, f32[128,128]{1,0:T(8,128)}, u32[]{:S(2)}) copy-start(f32[128,128]{1,0:T(8,128)} %param.13) | copy-start | bytes 196612
where the time goes:
time: 2060 us; the launch traced here: 2040 us
  waiting for transfers between devices  797 us (39%)
  matrix products  600 us (29%)
  local copies, waits for them, and re-layouts  481 us (23%)
  blocking collectives  92.7 us (4%)
  other arithmetic  38.1 us (2%)
  starting transfers between devices  31.4 us (2%)
    all_to_all x1, waiting for transfers between devices, body(): lax.all_to_all(returned, ('row', 'col'), split_axis=2, concat_axis=1, til...  403 us
    all_to_all x1, waiting for transfers between devices, body(): lax.all_to_all(stacked, ('row', 'col'), split_axis=1, concat_axis=2, tile...  394 us
    dot_general x2, matrix products, refine(): refined = jnp.einsum('cv,uv->cu', block, inverse, precision=PRECISE)  210 us
    dot_general x2, matrix products, refine(): local_gram = jnp.einsum('cv,cu->vu', block, block, precision=PRECISE)  149 us
    reshape x2, local copies, waits for them, and re-layouts, body(): returned.reshape(plane_count, row_devices, x_length, col_devices, z_lengt...  116 us
    reshape x2, local copies, waits for them, and re-layouts, body(): planes.reshape(x_length, plane_count, row_devices, col_devices, z_length,...  112 us
    psum x2, blocking collectives, refine(): gram_matrix = lax.psum(local_gram, ('row', 'col')) / cell_count  92.7 us
    dot_general x1, matrix products, body(): jnp.einsum('myrcnv,prm->ypcnv', planes, x_table, precision=PRECISE)  86.3 us
  transfers between devices with their start and end apart: 3, of which 2 were waited for; matrix products, arithmetic and copies ran while one was open for 2% of the time, Pallas kernels for 0%

commit v1 on v0

v1 whole, which is shorter than its diff:
```python
import functools
import math

import jax
import jax.numpy as jnp
from jax import lax
from jax.experimental import pallas as pl
from jax.experimental.pallas import tpu as pltpu
from jax.sharding import PartitionSpec as P

PRECISE = lax.Precision.HIGHEST
STEP_COEF = 10.0
VISCOSITY = 0.01
ALPHA_X = 0.5
BETA_Z = 1.0


def local_waves(points_count, first_index, length):
    indices = first_index + jnp.arange(length, dtype=jnp.int32)
    middle = points_count // 2
    return jnp.where(indices <= middle, indices, indices - middle).astype(jnp.float32)


def synthesis(points_count):
    points = jnp.arange(points_count, dtype=jnp.int32)[:, None]
    mode_index = jnp.arange(points_count, dtype=jnp.int32)[None, :]
    middle = points_count // 2
    wave_index = jnp.where(mode_index <= middle, mode_index, mode_index - middle)
    turn_count = (points * wave_index % points_count).astype(jnp.float32)
    angles = turn_count * (2.0 * math.pi / points_count)
    return jnp.where(mode_index <= middle, jnp.cos(angles), jnp.sin(angles))


def analysis(points_count):
    mode_index = jnp.arange(points_count, dtype=jnp.int32)
    middle = points_count // 2
    weights = jnp.where(
        (mode_index == 0) | (mode_index == middle),
        jnp.float32(1.0 / points_count),
        jnp.float32(2.0 / points_count),
    )
    return weights[:, None] * synthesis(points_count).T


def derivative_analysis(points_count, wave_scale):
    rows_index = jnp.arange(points_count, dtype=jnp.int32)[:, None]
    cols_index = jnp.arange(points_count, dtype=jnp.int32)[None, :]
    middle = points_count // 2
    rising = (cols_index == rows_index + middle) & (rows_index >= 1) & (rows_index < middle)
    falling = (rows_index == cols_index + middle) & (cols_index >= 1) & (cols_index < middle)
    rows_float = jnp.broadcast_to(rows_index.astype(jnp.float32), (points_count, points_count))
    cols_float = jnp.broadcast_to(cols_index.astype(jnp.float32), (points_count, points_count))
    derivative = jnp.where(rising, rows_float, jnp.float32(0.0)) - jnp.where(
        falling, cols_float, jnp.float32(0.0)
    )
    return -wave_scale * jnp.dot(derivative, analysis(points_count), precision=PRECISE)


def split_parts(value):
    high = value.astype(jnp.bfloat16)
    low = (value - high.astype(jnp.float32)).astype(jnp.bfloat16)
    return high, low


def parts_dot(left, right):
    left_high, left_low = left
    right_high, right_low = right
    dot = lambda a, b: jnp.dot(a, b, preferred_element_type=jnp.float32)
    return dot(left_high, right_high) + (dot(left_high, right_low) + dot(left_low, right_high))


def plane_kernel(vec_count, x_ref, speed_ref, sx_ref, sz_ref, az_ref, gx_ref, o_ref, rows, *halves):
    row_devices, col_devices, x_length, zv_length = x_ref.shape
    x_count = row_devices * x_length
    z_count = sz_ref.shape[0]
    if rows.shape[0] > x_count:
        rows[x_count:, :] = jnp.zeros((rows.shape[0] - x_count, zv_length), jnp.float32)
    for c in range(col_devices):
        for r in range(row_devices):
            rows[r * x_length : (r + 1) * x_length, :] = x_ref[r, c]
        for h, half in enumerate(halves):
            half[c * zv_length : (c + 1) * zv_length, :] = rows[h * 128 : (h + 1) * 128, :].T
    sx = split_parts(sx_ref[...])
    sz = split_parts(sz_ref[...])
    az = split_parts(az_ref[...])
    gx = split_parts(gx_ref[...])

    def step(group, carry):
        for u in range(2):
            where = pl.ds(group * 2 + u, z_count, stride=vec_count)
            field = jnp.concatenate([half[where, :] for half in halves], axis=1)
            field = parts_dot(split_parts(field), sx)
            field = parts_dot(sz, split_parts(field))
            field = field * speed_ref[...]
            field = parts_dot(az, split_parts(field))
            field = parts_dot(split_parts(field), gx)
            for h, half in enumerate(halves):
                half[where, :] = field[:, h * 128 : (h + 1) * 128]
        return carry

    lax.fori_loop(0, vec_count // 2, step, 0)
    for c in range(col_devices):
        for h, half in enumerate(halves):
            rows[h * 128 : (h + 1) * 128, :] = half[c * zv_length : (c + 1) * zv_length, :].T
        for r in range(row_devices):
            o_ref[r, c] = rows[r * x_length : (r + 1) * x_length, :]


def linear_terms(planes, speed, tables, vec_count):
    row_devices, col_devices, x_length, zv_length = planes.shape
    padded = tables[0].shape[0]
    z_count = tables[1].shape[0]
    flops = 2 * vec_count * 3 * 2 * (z_count * padded * padded + z_count * z_count * padded)
    return pl.pallas_call(
        functools.partial(plane_kernel, vec_count),
        out_shape=jax.ShapeDtypeStruct(planes.shape, jnp.float32),
        in_specs=[pl.BlockSpec(memory_space=pltpu.VMEM)] * 6,
        out_specs=pl.BlockSpec(memory_space=pltpu.VMEM),
        scratch_shapes=[pltpu.VMEM((padded, zv_length), jnp.float32)]
        + [pltpu.VMEM((z_count * vec_count, 128), jnp.float32)] * (padded // 128),
        cost_estimate=pl.CostEstimate(
            flops=flops, bytes_accessed=8 * planes.size, transcendentals=0
        ),
        compiler_params=pltpu.CompilerParams(vmem_limit_bytes=48 * 1024 * 1024),
    )(planes, speed, *tables)


def solve_kernel(chunks, q_ref, mask_ref, wave_ref, decay_ref, to_ref, from_ref, *rest):
    terms, (stepped_ref, gram_ref) = rest[:chunks], rest[chunks:]

    @pl.when(pl.program_id(0) == 0)
    def _():
        gram_ref[...] = jnp.zeros_like(gram_ref)

    nonlinear = jnp.concatenate([term[0] for term in terms], axis=0)
    right_side = STEP_COEF * q_ref[0] + nonlinear * mask_ref[0]
    eigen_part = parts_dot(split_parts(to_ref[...]), split_parts(right_side))
    eigen_part = eigen_part / (wave_ref[0] + decay_ref[...])
    stepped = parts_dot(split_parts(from_ref[...]), split_parts(eigen_part))
    stepped_ref[0] = stepped
    total = gram_ref[...]
    for g in range(stepped.shape[1] // 128):
        piece = stepped[:, g * 128 : (g + 1) * 128]
        total += lax.dot_general(
            piece,
            piece,
            (((0,), (0,)), ((), ())),
            precision=PRECISE,
            preferred_element_type=jnp.float32,
        )
    gram_ref[...] = total


def solve(tangents, mask_row, wave_row, decay_rates, to_eigen, from_eigen, terms):
    x_length, y_count, zv_length = tangents.shape
    whole = lambda *shape: pl.BlockSpec(shape, lambda m: (0,) * len(shape))
    one = lambda *shape: pl.BlockSpec((1,) + shape, lambda m: (m, 0, 0))
    return pl.pallas_call(
        functools.partial(solve_kernel, len(terms)),
        grid=(x_length,),
        out_shape=(
            jax.ShapeDtypeStruct(tangents.shape, jnp.float32),
            jax.ShapeDtypeStruct((128, 128), jnp.float32),
        ),
        in_specs=[
            one(y_count, zv_length),
            one(1, zv_length),
            one(1, zv_length),
            whole(y_count, 1),
            whole(y_count, y_count),
            whole(y_count, y_count),
        ]
        + [one(y_count // len(terms), zv_length)] * len(terms),
        out_specs=(one(y_count, zv_length), whole(128, 128)),
        compiler_params=pltpu.CompilerParams(vmem_limit_bytes=40 * 1024 * 1024),
    )(tangents, mask_row, wave_row, decay_rates[:, None], to_eigen, from_eigen, *terms)


def combine_kernel(x_ref, w_ref, o_ref):
    weights = split_parts(w_ref[...])
    for g in range(x_ref.shape[2] // 128):
        lanes = slice(g * 128, (g + 1) * 128)
        o_ref[0, :, lanes] = parts_dot(split_parts(x_ref[0, :, lanes]), weights)


def combine(stepped, weights):
    x_length, y_count, zv_length = stepped.shape
    one = pl.BlockSpec((1, y_count, zv_length), lambda m: (m, 0, 0))
    return pl.pallas_call(
        combine_kernel,
        grid=(x_length,),
        out_shape=jax.ShapeDtypeStruct(stepped.shape, jnp.float32),
        in_specs=[one, pl.BlockSpec((128, 128), lambda m: (0, 0))],
        out_specs=one,
    )(stepped, weights)


def body(tangents, base_flow, mode_mask, decay_rates, to_eigen, from_eigen):
    x_length, y_count, zv_length = tangents.shape
    z_length = base_flow.shape[2]
    vec_count = zv_length // z_length
    row_devices = lax.axis_size("row")
    col_devices = lax.axis_size("col")
    x_count = x_length * row_devices
    z_count = z_length * col_devices
    all_devices = row_devices * col_devices
    chunks = y_count // all_devices
    axes = ("row", "col")
    x_synthesis = synthesis(x_count)
    z_synthesis = synthesis(z_count)
    padded = -(-x_count // 128) * 128
    extra = padded - x_count
    widen = lambda table: jnp.pad(table, ((0, extra), (0, extra)))
    tables = (
        widen(x_synthesis.T),
        z_synthesis,
        analysis(z_count),
        widen(derivative_analysis(x_count, ALPHA_X).T),
    )
    exchange = lambda block: lax.all_to_all(block, axes, split_axis=0, concat_axis=0, tiled=True)
    base = jnp.transpose(base_flow.reshape(x_length, chunks, all_devices, z_length), (2, 1, 0, 3))
    base = exchange(base.reshape(all_devices, 1, chunks * x_length * z_length))
    base = base.reshape(row_devices, col_devices, chunks, x_length, z_length)
    base = jnp.transpose(base, (2, 0, 3, 1, 4)).reshape(chunks, x_count, z_count)
    speed = jnp.einsum("kmn,pm->kpn", base, x_synthesis, precision=PRECISE)
    speed = jnp.einsum("kpn,sn->ksp", speed, z_synthesis, precision=PRECISE)
    speed = jnp.pad(speed, ((0, 0), (0, 0), (0, extra)))
    received = []
    for k in range(chunks):
        piece = tangents[:, k * all_devices : (k + 1) * all_devices, :]
        received.append(exchange(jnp.transpose(piece, (1, 0, 2))))
    terms = []
    for k in range(chunks):
        planes = received[k].reshape(row_devices, col_devices, x_length, zv_length)
        returned = linear_terms(planes, speed[k], tables, vec_count)
        returned = exchange(returned.reshape(all_devices, x_length, zv_length))
        terms.append(jnp.transpose(returned, (1, 0, 2)))
    wave_x = ALPHA_X * local_waves(x_count, lax.axis_index("row") * x_length, x_length)
    wave_z = BETA_Z * local_waves(z_count, lax.axis_index("col") * z_length, z_length)
    wave_row = STEP_COEF + VISCOSITY * (wave_x[:, None] ** 2 + wave_z[None, :] ** 2)
    wave_row = jnp.repeat(wave_row, vec_count, axis=1)[:, None, :]
    mask_row = jnp.repeat(mode_mask.astype(jnp.float32), vec_count, axis=1)[:, None, :]
    stepped, local_gram = solve(
        tangents, mask_row, wave_row, decay_rates, to_eigen, from_eigen, terms
    )
    groups = 128 // vec_count
    local_gram = sum(
        local_gram[g * vec_count : (g + 1) * vec_count, g * vec_count : (g + 1) * vec_count]
        for g in range(groups)
    )
    gram_matrix = lax.psum(local_gram, axes) / (x_count * y_count * z_count)
    lower_factor = jnp.linalg.cholesky(gram_matrix)
    identity = jnp.eye(vec_count, dtype=jnp.float32)
    inverse = jax.scipy.linalg.solve_triangular(lower_factor, identity, lower=True)
    weights = jnp.kron(jnp.eye(groups, dtype=jnp.float32), inverse.T)
    return combine(stepped, weights), jnp.log(jnp.diagonal(lower_factor))


def solution(mesh):
    placed = (P("row", None, "col"), P("row", None, "col"), P("row", "col"), P(), P(), P())
    return jax.shard_map(
        body, mesh=mesh, in_specs=placed, out_specs=(P("row", None, "col"), P()), check_vma=False
    )
```

time: 2060 us -> 1060 us (0.51)
  matrix products: 600 us -> 5.04 us
  local copies, waits for them, and re-layouts: 481 us -> 89.6 us
  Pallas kernels: 0 us -> 258 us
  waiting for transfers between devices: 797 us -> 588 us
  blocking collectives: 92.7 us -> 42.4 us
  other arithmetic: 38.1 us -> 11 us
  starting transfers between devices: 31.4 us -> 56.5 us
    dot_general x12 -> x2, matrix products: 598 us -> 3.31 us  [the longest x1 1.66 us: body(): speed = jnp.einsum('kpn,sn->ksp', speed, z_synthesis, precision=PRECISE)]
    reshape x8 -> x4, local copies, waits for them, and re-layouts: 404 us -> 8.88 us  [the longest x2 3.91 us: body(): base = base.reshape(row_devices, col_devices, chunks, x_length, z_length)]
    pallas_call x0 -> x6, Pallas kernels: none -> 258 us  [the longest x4 168 us: linear_terms(): pl.pallas_call(functools.partial(plane_kernel, vec_count), out_shape=jax....]
    all_to_all x3 -> x9, waiting for transfers between devices: 797 us -> 588 us  [body(): lax.all_to_all(block, axes, split_axis=0, concat_axis=0, tiled=True)]
    psum x2 -> x1, blocking collectives: 92.7 us -> 42.4 us  [body(): gram_matrix = lax.psum(local_gram, axes) / (x_count * y_count * z_count)]
    all_to_all x3 -> x9, starting transfers between devices: 31.4 us -> 56.5 us  [body(): lax.all_to_all(block, axes, split_axis=0, concat_axis=0, tiled=True)]
    add x4 -> x2, other arithmetic: 21.2 us -> 0.15 us  [the longest x1 0.08 us: body(): sum((local_gram[g * vec_count:(g + 1) * vec_count, g * vec_count:(g + 1)...]
  transfers between devices with their start and end apart: 3 -> 9, of which waited for: 2 -> 8; matrix products, arithmetic and copies ran while one was open for 2% -> 7% of each run, Pallas kernels for 0% -> 16%
where the time goes in v1:
time: 1060 us; the launch traced here: 1050 us
  waiting for transfers between devices  588 us (55%)
  Pallas kernels  258 us (24%)
  local copies, waits for them, and re-layouts  89.6 us (8%)
  starting transfers between devices  56.5 us (5%)
  blocking collectives  42.4 us (4%)
  other arithmetic  11 us (1%)
    all_to_all x9, waiting for transfers between devices, body(): lax.all_to_all(block, axes, split_axis=0, concat_axis=0, tiled=True)  588 us
    pallas_call x4, Pallas kernels, linear_terms(): pl.pallas_call(functools.partial(plane_kernel, vec_count), out_shape=jax....  168 us
    pallas_call x1, Pallas kernels, solve(): pl.pallas_call(functools.partial(solve_kernel, len(terms)), grid=(x_lengt...  65 us
    all_to_all x9, starting transfers between devices, body(): lax.all_to_all(block, axes, split_axis=0, concat_axis=0, tiled=True)  56.5 us
    psum x1, blocking collectives, body(): gram_matrix = lax.psum(local_gram, axes) / (x_count * y_count * z_count)  42.4 us
    unnamed x23, local copies, waits for them, and re-layouts  37 us
    all_to_all x4, local copies, waits for them, and re-layouts, body(): lax.all_to_all(block, axes, split_axis=0, concat_axis=0, tiled=True)  27.2 us
    pallas_call x1, Pallas kernels, combine(): pl.pallas_call(combine_kernel, grid=(x_length,), out_shape=jax.ShapeDtype...  24.4 us
  transfers between devices with their start and end apart: 9, of which 8 were waited for; matrix products, arithmetic and copies ran while one was open for 7% of the time, Pallas kernels for 16%

profile of v1, /device:TPU:0, one launch (start us, length us, event | category | flops | bytes accessed | tf_op | source)
XLA Modules:
  0.0 1051.8 jit_solution(70978384531994019)
XLA Ops:
  0.6 1.5 copy.42
  3.1 2.4 reshape.166
  5.5 7.3 all-to-all-start.1
  12.8 12.1 %fusion.53 = (f32[24,32,1536]{2,1,0:T(8,128)S(1)}, f32[24,32,1536]{2,1,0:T(8,128)}, f32[24,32,1536]{2,1,0:T(8,128)}, f32[24,32,1536]{2,1,0:T(8,128)}) fusion(f32[24,128,1536]{2,1,0:T(8,128)} %q_ref.1), kind=kLoop, calls=%fused_computation.101 | loop fusion | bytes 37748736 | tf_op jit(solution)/shard_map/slice | solution.py:230
  24.9 4.9 copy.74
  29.8 5.9 all-to-all-start.7
  35.8 7.3 copy.75
  43.1 96.0 %all-to-all-done.7 = f32[32,24,1536]{2,1,0:T(8,128)} async-done(((f32[32,24,1536]{2,1,0:T(8,128)}), f32[32,24,1536]{2,1,0:T(8,128)}, u32[]{:S(2)}, u32[]{:S(2)}) %all-to-all-start.7) | async-done | bytes 4718624 | tf_op jit(solution)/shard_map/all_to_all | solution.py:220
  139.0 6.3 all-to-all-start.5
  145.3 7.3 copy.76
  152.6 95.9 %all-to-all-done.5 = f32[32,24,1536]{2,1,0:T(8,128)} async-done(((f32[32,24,1536]{2,1,0:T(8,128)}), f32[32,24,1536]{2,1,0:T(8,128)}, u32[]{:S(2)}, u32[]{:S(2)}) %all-to-all-start.5) | async-done | bytes 4718624 | tf_op jit(solution)/shard_map/all_to_all | solution.py:220
  248.5 6.0 all-to-all-start.3
  254.6 7.3 copy.77
  261.8 96.0 %all-to-all-done.3 = f32[32,24,1536]{2,1,0:T(8,128)} async-done(((f32[32,24,1536]{2,1,0:T(8,128)}), f32[32,24,1536]{2,1,0:T(8,128)}, u32[]{:S(2)}, u32[]{:S(2)}) %all-to-all-start.3) | async-done | bytes 4718624 | tf_op jit(solution)/shard_map/all_to_all | solution.py:220
  357.8 6.3 all-to-all-start
  365.7 1.7 broadcast_multiply_fusion.1
  367.4 2.3 reduce.6
  369.7 1.7 reshape.150
  371.5 2.2 copy.82
  373.7 2.6 reshape.151
  376.3 1.6 convolution_bitcast_fusion.1
  377.9 1.7 convolution_bitcast_fusion
  379.7 42.1 %shard_map.80 = f32[8,4,24,1536]{3,2,1,0:T(8,128)S(1)} custom-call(f32[8,4,24,1536]{3,2,1,0:T(8,128)} %bitcast.23.x_ref, f32[192,256]{1,0:T(8,128)S(1)} %get-tuple-element.12.speed_ref, f32[256,256]{1,0:T(8,128)S(1)} %pad.12.sx_ref, f32[192,192]{1,0:T(8,128)S(1)} %get-tuple-element.18.sz_ref, f32[192,192]{1,0:T(8,128)S(1)} %get-tuple-element.16.az_ref, ...), custom_call_target="tpu_custom_call" | custom-call | flops 8455716864 | bytes 9437184 | tf_op jit(solution)/shard_map/pallas_call | solution.py:114
  421.8 2.2 copy-done.3
  424.0 43.4 %all-to-all-done = f32[32,24,1536]{2,1,0:T(8,128)} async-done(((f32[32,24,1536]{2,1,0:T(8,128)}), f32[32,24,1536]{2,1,0:T(8,128)}, u32[]{:S(2)}, u32[]{:S(2)}) %all-to-all-start) | async-done | bytes 4718624 | tf_op jit(solution)/shard_map/all_to_all | solution.py:220
  467.3 6.2 all-to-all-start.8
  473.6 42.1 %shard_map.79 = f32[8,4,24,1536]{3,2,1,0:T(8,128)S(1)} custom-call(f32[8,4,24,1536]{3,2,1,0:T(8,128)} %bitcast.18.x_ref, f32[192,256]{1,0:T(8,128)S(1)} %get-tuple-element.14.speed_ref, f32[256,256]{1,0:T(8,128)S(1)} %pad.12.sx_ref, f32[192,192]{1,0:T(8,128)S(1)} %get-tuple-element.18.sz_ref, f32[192,192]{1,0:T(8,128)S(1)} %get-tuple-element.16.az_ref, ...), custom_call_target="tpu_custom_call" | custom-call | flops 8455716864 | bytes 9437184 | tf_op jit(solution)/shard_map/pallas_call | solution.py:114
  515.7 2.2 copy-done.4
  517.9 58.9 %all-to-all-done.8 = f32[32,24,1536]{2,1,0:T(8,128)} async-done(((f32[32,24,1536]{2,1,0:T(8,128)}), f32[32,24,1536]{2,1,0:T(8,128)}, u32[]{:S(2)}, u32[]{:S(2)}) %all-to-all-start.8) | async-done | bytes 4718624 | tf_op jit(solution)/shard_map/all_to_all | solution.py:220
  576.8 6.0 all-to-all-start.6
  582.9 42.1 %shard_map.78 = f32[8,4,24,1536]{3,2,1,0:T(8,128)S(1)} custom-call(f32[8,4,24,1536]{3,2,1,0:T(8,128)} %bitcast.13.x_ref, f32[192,256]{1,0:T(8,128)S(1)} %get-tuple-element.13.speed_ref, f32[256,256]{1,0:T(8,128)S(1)} %pad.12.sx_ref, f32[192,192]{1,0:T(8,128)S(1)} %get-tuple-element.18.sz_ref, f32[192,192]{1,0:T(8,128)S(1)} %get-tuple-element.16.az_ref, ...), custom_call_target="tpu_custom_call" | custom-call | flops 8455716864 | bytes 9437184 | tf_op jit(solution)/shard_map/pallas_call | solution.py:114
  625.0 2.2 copy-done.2
  627.2 58.9 %all-to-all-done.6 = f32[32,24,1536]{2,1,0:T(8,128)} async-done(((f32[32,24,1536]{2,1,0:T(8,128)}), f32[32,24,1536]{2,1,0:T(8,128)}, u32[]{:S(2)}, u32[]{:S(2)}) %all-to-all-start.6) | async-done | bytes 4718624 | tf_op jit(solution)/shard_map/all_to_all | solution.py:220
  686.1 6.0 all-to-all-start.4
  692.2 42.1 %shard_map.77 = f32[8,4,24,1536]{3,2,1,0:T(8,128)S(1)} custom-call(f32[8,4,24,1536]{3,2,1,0:T(8,128)} %bitcast.2.x_ref, f32[192,256]{1,0:T(8,128)S(1)} %get-tuple-element.15.speed_ref, f32[256,256]{1,0:T(8,128)S(1)} %pad.12.sx_ref, f32[192,192]{1,0:T(8,128)S(1)} %get-tuple-element.18.sz_ref, f32[192,192]{1,0:T(8,128)S(1)} %get-tuple-element.16.az_ref, ...), custom_call_target="tpu_custom_call" | custom-call | flops 8455716864 | bytes 9437184 | tf_op jit(solution)/shard_map/pallas_call | solution.py:114
  734.3 2.2 copy-done.1
  736.4 59.0 %all-to-all-done.4 = f32[32,24,1536]{2,1,0:T(8,128)} async-done(((f32[32,24,1536]{2,1,0:T(8,128)}), f32[32,24,1536]{2,1,0:T(8,128)}, u32[]{:S(2)}, u32[]{:S(2)}) %all-to-all-start.4) | async-done | bytes 4718624 | tf_op jit(solution)/shard_map/all_to_all | solution.py:220
  795.4 6.3 all-to-all-start.2
  802.9 7.3 copy.78
  810.2 7.3 copy.79
  817.5 7.2 copy.80
  824.7 80.0 %all-to-all-done.2 = f32[32,24,1536]{2,1,0:T(8,128)} async-done(((f32[32,24,1536]{2,1,0:T(8,128)}), f32[32,24,1536]{2,1,0:T(8,128)}, u32[]{:S(2)}, u32[]{:S(2)}) %all-to-all-start.2) | async-done | bytes 4718624 | tf_op jit(solution)/shard_map/all_to_all | solution.py:220
  904.7 5.5 copy.81
  910.2 65.0 %shard_map.81 = (f32[24,128,1536]{2,1,0:T(8,128)}, f32[128,128]{1,0:T(8,128)S(1)}) custom-call(f32[24,128,1536]{2,1,0:T(8,128)} %q_ref.1, f32[24,1,1536]{2,1,0:T(1,128)S(1)} %broadcast_in_dim_reshape.8.mask_ref, f32[24,1,1536]{2,1,0:T(1,128)S(1)} %broadcast_in_dim_reshape.9.wave_ref, f32[128,1]{1,0:T(8,128)S(1)} %copy.55.decay_ref, ...), custom_call_target="tpu_custom_call" | custom-call | tf_op jit(solution)/shard_map/pallas_call | solution.py:158
  975.4 42.4 %psum.7 = f32[32,32]{0,1:T(8,128)S(1)} all-reduce(f32[32,32]{0,1:T(8,128)S(1)} %slice_add_fusion), channel_id=1, replica_groups=mesh['row'=8,'col'=4] {'row','col'}, use_global_device_ids=true, to_apply=%region_0.1 | all-reduce | flops 1024 | bytes 8192 | tf_op jit(solution)/shard_map/psum | solution.py:251
  1017.8 2.9 cholesky.14
  1022.1 2.4 custom-call.7
  1026.9 24.4 %shard_map.82 = f32[24,128,1536]{2,1,0:T(8,128)} custom-call(f32[24,128,1536]{2,1,0:T(8,128)} %get-tuple-element.4.x_ref, f32[128,128]{1,0:T(8,128)} %mul.231.w_ref), custom_call_target="tpu_custom_call" | custom-call | tf_op jit(solution)/shard_map/pallas_call | solution.py:189
  (49 shorter events, 7.7 us)
Async XLA Ops:
  5.5 24.4 %all-to-all-start.1 = ((f32[32,1,4608]{2,1,0:T(1,128)}), f32[32,1,4608]{2,1,0:T(1,128)S(1)}, u32[]{:S(2)}, u32[]{:S(2)}) async-start(f32[32,1,4608]{2,1,0:T(1,128)} %reshape.166), calls=%async_computation.1 | async-start | bytes 1179648 | tf_op jit(solution)/shard_map/all_to_all | solution.py:220
  29.8 109.2 %all-to-all-start.7 = ((f32[32,24,1536]{2,1,0:T(8,128)}), f32[32,24,1536]{2,1,0:T(8,128)}, u32[]{:S(2)}, u32[]{:S(2)}) async-start(f32[32,24,1536]{2,1,0:T(8,128)} %bitcast.79), calls=%async_computation.7 | async-start | bytes 9437184 | tf_op jit(solution)/shard_map/all_to_all | solution.py:220
  139.0 109.5 %all-to-all-start.5 = ((f32[32,24,1536]{2,1,0:T(8,128)}), f32[32,24,1536]{2,1,0:T(8,128)}, u32[]{:S(2)}, u32[]{:S(2)}) async-start(f32[32,24,1536]{2,1,0:T(8,128)} %bitcast.80), calls=%async_computation.5 | async-start | bytes 9437184 | tf_op jit(solution)/shard_map/all_to_all | solution.py:220
  248.5 109.3 %all-to-all-start.3 = ((f32[32,24,1536]{2,1,0:T(8,128)}), f32[32,24,1536]{2,1,0:T(8,128)}, u32[]{:S(2)}, u32[]{:S(2)}) async-start(f32[32,24,1536]{2,1,0:T(8,128)} %bitcast.78), calls=%async_computation.3 | async-start | bytes 9437184 | tf_op jit(solution)/shard_map/all_to_all | solution.py:220
  357.8 109.5 %all-to-all-start = ((f32[32,24,1536]{2,1,0:T(8,128)}), f32[32,24,1536]{2,1,0:T(8,128)}, u32[]{:S(2)}, u32[]{:S(2)}) async-start(f32[32,24,1536]{2,1,0:T(8,128)} %bitcast.77), calls=%async_computation | async-start | bytes 9437184 | tf_op jit(solution)/shard_map/all_to_all | solution.py:220
  421.7 2.2 copy-start.3
  467.3 109.5 %all-to-all-start.8 = ((f32[32,24,1536]{2,1,0:T(8,128)}), f32[32,24,1536]{2,1,0:T(8,128)}, u32[]{:S(2)}, u32[]{:S(2)}) async-start(f32[32,24,1536]{2,1,0:T(8,128)} %bitcast.75), calls=%async_computation.8 | async-start | bytes 9437184 | tf_op jit(solution)/shard_map/all_to_all | solution.py:220
  515.7 2.2 copy-start.4
  576.8 109.3 %all-to-all-start.6 = ((f32[32,24,1536]{2,1,0:T(8,128)}), f32[32,24,1536]{2,1,0:T(8,128)}, u32[]{:S(2)}, u32[]{:S(2)}) async-start(f32[32,24,1536]{2,1,0:T(8,128)} %bitcast.76), calls=%async_computation.6 | async-start | bytes 9437184 | tf_op jit(solution)/shard_map/all_to_all | solution.py:220
  624.9 2.2 copy-start.2
  686.1 109.3 %all-to-all-start.4 = ((f32[32,24,1536]{2,1,0:T(8,128)}), f32[32,24,1536]{2,1,0:T(8,128)}, u32[]{:S(2)}, u32[]{:S(2)}) async-start(f32[32,24,1536]{2,1,0:T(8,128)} %bitcast.74), calls=%async_computation.4 | async-start | bytes 9437184 | tf_op jit(solution)/shard_map/all_to_all | solution.py:220
  734.2 2.2 copy-start.1
  795.4 6.9 copy-start.7
  795.4 7.4 copy-start.8
  795.4 109.3 %all-to-all-start.2 = ((f32[32,24,1536]{2,1,0:T(8,128)}), f32[32,24,1536]{2,1,0:T(8,128)}, u32[]{:S(2)}, u32[]{:S(2)}) async-start(f32[32,24,1536]{2,1,0:T(8,128)} %bitcast.73), calls=%async_computation.2 | async-start | bytes 9437184 | tf_op jit(solution)/shard_map/all_to_all | solution.py:220
  824.7 85.5 %copy-start.5 = (f32[128,128]{1,0:T(8,128)S(1)}, f32[128,128]{1,0:T(8,128)}, u32[]{:S(2)}) copy-start(f32[128,128]{1,0:T(8,128)} %to_ref.1) | copy-start | bytes 196612
  824.7 85.5 %copy-start.6 = (f32[128,128]{1,0:T(8,128)S(1)}, f32[128,128]{1,0:T(8,128)}, u32[]{:S(2)}) copy-start(f32[128,128]{1,0:T(8,128)} %from_ref.1) | copy-start | bytes 196612
  904.7 5.5 copy-start

commit v2 on v1

--- a/solution.py
+++ b/solution.py
@@ -7,6 +7,7 @@
 from jax.experimental import pallas as pl
 from jax.experimental.pallas import tpu as pltpu
 from jax.sharding import PartitionSpec as P
+
 
 PRECISE = lax.Precision.HIGHEST
 STEP_COEF = 10.0
@@ -70,14 +71,14 @@
 
 
 def plane_kernel(vec_count, x_ref, speed_ref, sx_ref, sz_ref, az_ref, gx_ref, o_ref, rows, *halves):
-    row_devices, col_devices, x_length, zv_length = x_ref.shape
+    row_devices, col_devices, _, x_length, zv_length = x_ref.shape
     x_count = row_devices * x_length
     z_count = sz_ref.shape[0]
     if rows.shape[0] > x_count:
         rows[x_count:, :] = jnp.zeros((rows.shape[0] - x_count, zv_length), jnp.float32)
     for c in range(col_devices):
         for r in range(row_devices):
-            rows[r * x_length : (r + 1) * x_length, :] = x_ref[r, c]
+            rows[r * x_length : (r + 1) * x_length, :] = x_ref[r, c, 0]
         for h, half in enumerate(halves):
             half[c * zv_length : (c + 1) * zv_length, :] = rows[h * 128 : (h + 1) * 128, :].T
     sx = split_parts(sx_ref[...])
@@ -91,7 +92,7 @@
             field = jnp.concatenate([half[where, :] for half in halves], axis=1)
             field = parts_dot(split_parts(field), sx)
             field = parts_dot(sz, split_parts(field))
-            field = field * speed_ref[...]
+            field = field * speed_ref[0]
             field = parts_dot(az, split_parts(field))
             field = parts_dot(split_parts(field), gx)
             for h, half in enumerate(halves):
@@ -103,19 +104,24 @@
         for h, half in enumerate(halves):
             rows[h * 128 : (h + 1) * 128, :] = half[c * zv_length : (c + 1) * zv_length, :].T
         for r in range(row_devices):
-            o_ref[r, c] = rows[r * x_length : (r + 1) * x_length, :]
+            o_ref[r, c, 0] = rows[r * x_length : (r + 1) * x_length, :]
 
 
 def linear_terms(planes, speed, tables, vec_count):
-    row_devices, col_devices, x_length, zv_length = planes.shape
+    row_devices, col_devices, plane_count, x_length, zv_length = planes.shape
     padded = tables[0].shape[0]
     z_count = tables[1].shape[0]
-    flops = 2 * vec_count * 3 * 2 * (z_count * padded * padded + z_count * z_count * padded)
+    flops = 2 * plane_count * vec_count * 6 * z_count * padded * (padded + z_count)
+    field = pl.BlockSpec(
+        (row_devices, col_devices, 1, x_length, zv_length), lambda l: (0, 0, l, 0, 0)
+    )
     return pl.pallas_call(
         functools.partial(plane_kernel, vec_count),
+        grid=(plane_count,),
         out_shape=jax.ShapeDtypeStruct(planes.shape, jnp.float32),
-        in_specs=[pl.BlockSpec(memory_space=pltpu.VMEM)] * 6,
-        out_specs=pl.BlockSpec(memory_space=pltpu.VMEM),
+        in_specs=[field, pl.BlockSpec((1,) + speed.shape[1:], lambda l: (l, 0, 0))]
+        + [pl.BlockSpec(table.shape, lambda l: (0, 0)) for table in tables],
+        out_specs=field,
         scratch_shapes=[pltpu.VMEM((padded, zv_length), jnp.float32)]
         + [pltpu.VMEM((z_count * vec_count, 128), jnp.float32)] * (padded // 128),
         cost_estimate=pl.CostEstimate(
@@ -125,55 +131,91 @@
     )(planes, speed, *tables)
 
 
-def solve_kernel(chunks, q_ref, mask_ref, wave_ref, decay_ref, to_ref, from_ref, *rest):
-    terms, (stepped_ref, gram_ref) = rest[:chunks], rest[chunks:]
-
-    @pl.when(pl.program_id(0) == 0)
-    def _():
-        gram_ref[...] = jnp.zeros_like(gram_ref)
-
-    nonlinear = jnp.concatenate([term[0] for term in terms], axis=0)
-    right_side = STEP_COEF * q_ref[0] + nonlinear * mask_ref[0]
-    eigen_part = parts_dot(split_parts(to_ref[...]), split_parts(right_side))
-    eigen_part = eigen_part / (wave_ref[0] + decay_ref[...])
-    stepped = parts_dot(split_parts(from_ref[...]), split_parts(eigen_part))
-    stepped_ref[0] = stepped
-    total = gram_ref[...]
-    for g in range(stepped.shape[1] // 128):
-        piece = stepped[:, g * 128 : (g + 1) * 128]
-        total += lax.dot_general(
-            piece,
-            piece,
-            (((0,), (0,)), ((), ())),
-            precision=PRECISE,
-            preferred_element_type=jnp.float32,
-        )
-    gram_ref[...] = total
-
-
-def solve(tangents, mask_row, wave_row, decay_rates, to_eigen, from_eigen, terms):
+def prepare_kernel(q_ref, mask_ref, to_ref, *rest):
+    terms, o_ref = rest[:-1], rest[-1]
+    right_side = STEP_COEF * q_ref[0]
+    if terms:
+        added = jnp.concatenate([term[0] for term in terms], axis=0) * mask_ref[0]
+        known = added.shape[0]
+        right_side = jnp.concatenate([right_side[:known] + added, right_side[known:]], axis=0)
+    o_ref[0] = parts_dot(split_parts(to_ref[...]), split_parts(right_side))
+
+
+def prepare(tangents, mask_row, to_eigen, terms):
     x_length, y_count, zv_length = tangents.shape
-    whole = lambda *shape: pl.BlockSpec(shape, lambda m: (0,) * len(shape))
     one = lambda *shape: pl.BlockSpec((1,) + shape, lambda m: (m, 0, 0))
     return pl.pallas_call(
-        functools.partial(solve_kernel, len(terms)),
+        prepare_kernel,
         grid=(x_length,),
-        out_shape=(
-            jax.ShapeDtypeStruct(tangents.shape, jnp.float32),
-            jax.ShapeDtypeStruct((128, 128), jnp.float32),
-        ),
+        out_shape=jax.ShapeDtypeStruct(tangents.shape, jnp.float32),
         in_specs=[
             one(y_count, zv_length),
             one(1, zv_length),
-            one(1, zv_length),
+            pl.BlockSpec((y_count, y_count), lambda m: (0, 0)),
+        ]
+        + [one(term.shape[1], zv_length) for term in terms],
+        out_specs=one(y_count, zv_length),
+        cost_estimate=pl.CostEstimate(
+            flops=6 * y_count * tangents.size, bytes_accessed=10 * tangents.size, transcendentals=0
+        ),
+        compiler_params=pltpu.CompilerParams(vmem_limit_bytes=16 * 1024 * 1024),
+    )(tangents, mask_row, to_eigen, *terms)
+
+
+def finish_kernel(
+    eigen_ref, mask_ref, wave_ref, decay_ref, to_ref, from_ref, term_ref, stepped_ref, high_ref, cross_ref
+):
+    @pl.when(pl.program_id(0) == 0)
+    def _():
+        high_ref[...] = jnp.zeros_like(high_ref)
+        cross_ref[...] = jnp.zeros_like(cross_ref)
+
+    into, back = split_parts(to_ref[...]), split_parts(from_ref[...])
+    highs, lows = [], []
+    for b in range(eigen_ref.shape[0]):
+        late = parts_dot(into, split_parts(term_ref[b] * mask_ref[b]))
+        eigen_part = (eigen_ref[b] + late) / (wave_ref[b] + decay_ref[...])
+        stepped = parts_dot(back, split_parts(eigen_part))
+        stepped_ref[b] = stepped
+        high, low = split_parts(stepped)
+        highs.append(high)
+        lows.append(low)
+    high, low = jnp.concatenate(highs, axis=0), jnp.concatenate(lows, axis=0)
+    inner = lambda a, b: lax.dot_general(
+        a, b, (((0,), (0,)), ((), ())), preferred_element_type=jnp.float32
+    )
+    high_total, cross_total = high_ref[...], cross_ref[...]
+    for g in range(high.shape[1] // 128):
+        lanes = slice(g * 128, (g + 1) * 128)
+        high_total += inner(high[:, lanes], high[:, lanes])
+        cross_total += inner(high[:, lanes], low[:, lanes])
+    high_ref[...] = high_total
+    cross_ref[...] = cross_total
+
+
+def finish(eigen_sum, mask_row, wave_row, decay_rates, to_late, from_eigen, term):
+    x_length, y_count, zv_length = eigen_sum.shape
+    batch = 2 if x_length % 2 == 0 else 1
+    whole = lambda *shape: pl.BlockSpec(shape, lambda m: (0,) * len(shape))
+    some = lambda *shape: pl.BlockSpec((batch,) + shape, lambda m: (m, 0, 0))
+    square = jax.ShapeDtypeStruct((128, 128), jnp.float32)
+    stepped, high, cross = pl.pallas_call(
+        finish_kernel,
+        grid=(x_length // batch,),
+        out_shape=(jax.ShapeDtypeStruct(eigen_sum.shape, jnp.float32), square, square),
+        in_specs=[
+            some(y_count, zv_length),
+            some(1, zv_length),
+            some(1, zv_length),
             whole(y_count, 1),
+            whole(*to_late.shape),
             whole(y_count, y_count),
-            whole(y_count, y_count),
-        ]
-        + [one(y_count // len(terms), zv_length)] * len(terms),
-        out_specs=(one(y_count, zv_length), whole(128, 128)),
-        compiler_params=pltpu.CompilerParams(vmem_limit_bytes=40 * 1024 * 1024),
-    )(tangents, mask_row, wave_row, decay_rates[:, None], to_eigen, from_eigen, *terms)
+            some(term.shape[1], zv_length),
+        ],
+        out_specs=(some(y_count, zv_length), whole(128, 128), whole(128, 128)),
+        compiler_params=pltpu.CompilerParams(vmem_limit_bytes=20 * 1024 * 1024),
+    )(eigen_sum, mask_row, wave_row, decay_rates[:, None], to_late, from_eigen, term)
+    return stepped, high + cross + cross.T
 
 
 def combine_kernel(x_ref, w_ref, o_ref):
@@ -192,6 +234,7 @@
         out_shape=jax.ShapeDtypeStruct(stepped.shape, jnp.float32),
         in_specs=[one, pl.BlockSpec((128, 128), lambda m: (0, 0))],
         out_specs=one,
+        compiler_params=pltpu.CompilerParams(vmem_limit_bytes=12 * 1024 * 1024),
     )(stepped, weights)
 
 
@@ -204,7 +247,10 @@
     x_count = x_length * row_devices
     z_count = z_length * col_devices
     all_devices = row_devices * col_devices
-    chunks = y_count // all_devices
+    device_planes = y_count // all_devices
+    per_chunk = 2 if device_planes % 2 == 0 else 1
+    chunks = device_planes // per_chunk
+    chunk_rows = per_chunk * all_devices
     axes = ("row", "col")
     x_synthesis = synthesis(x_count)
     z_synthesis = synthesis(z_count)
@@ -218,37 +264,45 @@
         widen(derivative_analysis(x_count, ALPHA_X).T),
     )
     exchange = lambda block: lax.all_to_all(block, axes, split_axis=0, concat_axis=0, tiled=True)
-    base = jnp.transpose(base_flow.reshape(x_length, chunks, all_devices, z_length), (2, 1, 0, 3))
-    base = exchange(base.reshape(all_devices, 1, chunks * x_length * z_length))
-    base = base.reshape(row_devices, col_devices, chunks, x_length, z_length)
-    base = jnp.transpose(base, (2, 0, 3, 1, 4)).reshape(chunks, x_count, z_count)
+    received = []
+    source = tangents
+    for k in range(chunks):
+        piece = source[:, k * chunk_rows : (k + 1) * chunk_rows, :]
+        piece = jnp.transpose(piece, (1, 0, 2)).reshape(all_devices, per_chunk * x_length, zv_length)
+        if k == 0:
+            source, piece = lax.optimization_barrier((source, piece))
+        received.append(exchange(piece))
+    base = base_flow.reshape(x_length, chunks, all_devices, per_chunk, z_length)
+    base = jnp.transpose(base, (2, 1, 3, 0, 4))
+    base = exchange(base.reshape(all_devices, 1, device_planes * x_length * z_length))
+    base = base.reshape(row_devices, col_devices, device_planes, x_length, z_length)
+    base = jnp.transpose(base, (2, 0, 3, 1, 4)).reshape(device_planes, x_count, z_count)
     speed = jnp.einsum("kmn,pm->kpn", base, x_synthesis, precision=PRECISE)
     speed = jnp.einsum("kpn,sn->ksp", speed, z_synthesis, precision=PRECISE)
     speed = jnp.pad(speed, ((0, 0), (0, 0), (0, extra)))
-    received = []
-    for k in range(chunks):
-        piece = tangents[:, k * all_devices : (k + 1) * all_devices, :]
-        received.append(exchange(jnp.transpose(piece, (1, 0, 2))))
+    speed = speed.reshape(chunks, per_chunk, z_count, padded)
     terms = []
     for k in range(chunks):
-        planes = received[k].reshape(row_devices, col_devices, x_length, zv_length)
+        planes = received[k].reshape(row_devices, col_devices, per_chunk, x_length, zv_length)
         returned = linear_terms(planes, speed[k], tables, vec_count)
-        returned = exchange(returned.reshape(all_devices, x_length, zv_length))
-        terms.append(jnp.transpose(returned, (1, 0, 2)))
+        returned = exchange(returned.reshape(all_devices, per_chunk * x_length, zv_length))
+        terms.append(jnp.transpose(returned.reshape(chunk_rows, x_length, zv_length), (1, 0, 2)))
     wave_x = ALPHA_X * local_waves(x_count, lax.axis_index("row") * x_length, x_length)
     wave_z = BETA_Z * local_waves(z_count, lax.axis_index("col") * z_length, z_length)
     wave_row = STEP_COEF + VISCOSITY * (wave_x[:, None] ** 2 + wave_z[None, :] ** 2)
     wave_row = jnp.repeat(wave_row, vec_count, axis=1)[:, None, :]
     mask_row = jnp.repeat(mode_mask.astype(jnp.float32), vec_count, axis=1)[:, None, :]
-    stepped, local_gram = solve(
-        tangents, mask_row, wave_row, decay_rates, to_eigen, from_eigen, terms
+    eigen_sum = prepare(tangents, mask_row, to_eigen, terms[:-1])
+    to_late = to_eigen[:, y_count - chunk_rows :]
+    stepped, local_gram = finish(
+        eigen_sum, mask_row, wave_row, decay_rates, to_late, from_eigen, terms[-1]
     )
     groups = 128 // vec_count
     local_gram = sum(
         local_gram[g * vec_count : (g + 1) * vec_count, g * vec_count : (g + 1) * vec_count]
         for g in range(groups)
     )
-    gram_matrix = lax.psum(local_gram, axes) / (x_count * y_count * z_count)
+    gram_matrix = lax.psum(lax.psum(local_gram, "row"), "col") / (x_count * y_count * z_count)
     lower_factor = jnp.linalg.cholesky(gram_matrix)
     identity = jnp.eye(vec_count, dtype=jnp.float32)
     inverse = jax.scipy.linalg.solve_triangular(lower_factor, identity, lower=True)

time: 1060 us -> 1030 us (0.972)
  Pallas kernels: 258 us -> 233 us
  starting transfers between devices: 56.5 us -> 39.6 us
  waiting for transfers between devices: 588 us -> 599 us
    all_to_all x4 -> x0, local copies, waits for them, and re-layouts: 27.2 us -> none  [body(): lax.all_to_all(block, axes, split_axis=0, concat_axis=0, tiled=True)]
    reshape x4 -> x6, local copies, waits for them, and re-layouts: 8.88 us -> 29.6 us  [the longest x2 22.2 us: body(): returned.reshape(chunk_rows, x_length, zv_length)]
    pallas_call x5 -> x4, Pallas kernels: 233 us -> 216 us  [the longest x2 169 us: linear_terms(): pl.pallas_call(functools.partial(plane_kernel, vec_count), grid=(plane_co...]
    optimization_barrier x0 -> x1, local copies, waits for them, and re-layouts: none -> 17 us  [body(): source, piece = lax.optimization_barrier((source, piece))]
    all_to_all x9 -> x5, starting transfers between devices: 56.5 us -> 39.6 us  [body(): lax.all_to_all(block, axes, split_axis=0, concat_axis=0, tiled=True)]
    all_to_all x9 -> x5, waiting for transfers between devices: 588 us -> 599 us  [body(): lax.all_to_all(block, axes, split_axis=0, concat_axis=0, tiled=True)]
    psum x1 -> x2, blocking collectives: 42.4 us -> 44.8 us  [the longest x1 25.1 us: body(): lax.psum(local_gram, 'row')]
    unnamed x23 -> x22, local copies, waits for them, and re-layouts: 37 us -> 35.4 us
  transfers between devices with their start and end apart: 9 -> 5, of which waited for: 8 -> 5; matrix products, arithmetic and copies ran while one was open for 7% -> 6% of each run, Pallas kernels for 16% -> 16%
where the time goes in v2:
time: 1030 us
  waiting for transfers between devices  599 us (58%)
  Pallas kernels  233 us (23%)
  local copies, waits for them, and re-layouts  93.3 us (9%)
  blocking collectives  44.8 us (4%)
  starting transfers between devices  39.6 us (4%)
    all_to_all x5, waiting for transfers between devices, body(): lax.all_to_all(block, axes, split_axis=0, concat_axis=0, tiled=True)  599 us
    pallas_call x2, Pallas kernels, linear_terms(): pl.pallas_call(functools.partial(plane_kernel, vec_count), grid=(plane_co...  169 us
    all_to_all x5, starting transfers between devices, body(): lax.all_to_all(block, axes, split_axis=0, concat_axis=0, tiled=True)  39.6 us
    unnamed x22, local copies, waits for them, and re-layouts  35.4 us
    pallas_call x1, Pallas kernels, finish(): pl.pallas_call(finish_kernel, grid=(x_length // batch,), out_shape=(jax.S...  26.6 us
    psum x1, blocking collectives, body(): lax.psum(local_gram, 'row')  25.1 us
    reshape x2, local copies, waits for them, and re-layouts, body(): returned.reshape(chunk_rows, x_length, zv_length)  22.2 us
  transfers between devices with their start and end apart: 5, of which 5 were waited for; matrix products, arithmetic and copies ran while one was open for 6% of the time, Pallas kernels for 16%

profile of v2, /device:TPU:0, one launch (start us, length us, event | category | flops | bytes accessed | tf_op | source)
XLA Modules:
  0.0 1026.1 jit_solution(1243492285412753532)
XLA Ops:
  0.6 1.6 copy.27
  2.4 2.4 reshape.171
  4.8 7.3 all-to-all-start.1
  12.2 3.7 slice-done
  15.8 9.2 copy.41
  25.0 2.6 all-to-all-done.1
  27.7 0.8 copy-done.6
  28.5 4.6 all-to-all-start
  33.1 17.0 %copy.33 = f32[24,128,1536]{2,0,1:T(8,128)S(1)} copy(f32[24,128,1536]{2,1,0:T(8,128)} %q_ref.1) | data formatting | bytes 37748736 | tf_op jit(solution)/shard_map/optimization_barrier | solution.py:273
  50.1 4.5 slice.52
  54.6 182.1 %all-to-all-done = f32[32,48,1536]{2,1,0:T(8,128)} async-done(((f32[32,48,1536]{2,1,0:T(8,128)}), f32[32,48,1536]{2,1,0:T(8,128)}, u32[]{:S(2)}, u32[]{:S(2)}) %all-to-all-start) | async-done | bytes 9437216 | tf_op jit(solution)/shard_map/all_to_all | solution.py:266
  236.7 9.2 all-to-all-start.3
  246.0 1.5 convolution_multiply_fusion
  247.5 1.7 broadcast_multiply_fusion.1
  249.2 1.4 reduce.6
  250.6 0.7 reshape.156
  251.3 2.2 copy.47
  253.5 2.1 reshape.157
  255.6 1.6 convolution_bitcast_fusion.1
  257.3 1.7 convolution_bitcast_fusion
  259.0 84.5 %shard_map.77 = f32[8,4,2,24,1536]{4,3,2,1,0:T(8,128)} custom-call(f32[8,4,2,24,1536]{4,3,2,1,0:T(8,128)} %bitcast.2.x_ref, f32[2,192,256]{2,1,0:T(8,128)S(1)} %get-tuple-element.15.speed_ref, f32[256,256]{1,0:T(8,128)S(1)} %pad.12.sx_ref, f32[192,192]{1,0:T(8,128)S(1)} %get-tuple-element.18.sz_ref, f32[192,192]{1,0:T(8,128)S(1)} %get-tuple-element.16.az_ref, ...), custom_call_target="tpu_custom_call" | custom-call | flops 16911433728 | bytes 18874368 | tf_op jit(solution)/shard_map/pallas_call | solution.py:118
  343.5 106.1 %all-to-all-done.3 = f32[32,48,1536]{2,1,0:T(8,128)} async-done(((f32[32,48,1536]{2,1,0:T(8,128)}), f32[32,48,1536]{2,1,0:T(8,128)}, u32[]{:S(2)}, u32[]{:S(2)}) %all-to-all-start.3) | async-done | bytes 9437216 | tf_op jit(solution)/shard_map/all_to_all | solution.py:266
  449.6 9.2 all-to-all-start.2
  458.8 84.3 %shard_map.79 = f32[8,4,2,24,1536]{4,3,2,1,0:T(8,128)} custom-call(f32[8,4,2,24,1536]{4,3,2,1,0:T(8,128)} %bitcast.15.x_ref, f32[2,192,256]{2,1,0:T(8,128)S(1)} %get-tuple-element.14.speed_ref, f32[256,256]{1,0:T(8,128)S(1)} %pad.12.sx_ref, f32[192,192]{1,0:T(8,128)S(1)} %get-tuple-element.18.sz_ref, f32[192,192]{1,0:T(8,128)S(1)} %get-tuple-element.16.az_ref, ...), custom_call_target="tpu_custom_call" | custom-call | flops 16911433728 | bytes 18874368 | tf_op jit(solution)/shard_map/pallas_call | solution.py:118
  543.0 119.4 %all-to-all-done.2 = f32[32,48,1536]{2,1,0:T(8,128)} async-done(((f32[32,48,1536]{2,1,0:T(8,128)}), f32[32,48,1536]{2,1,0:T(8,128)}, u32[]{:S(2)}, u32[]{:S(2)}) %all-to-all-start.2) | async-done | bytes 9437216 | tf_op jit(solution)/shard_map/all_to_all | solution.py:266
  662.4 9.3 all-to-all-start.4
  672.0 0.3 broadcast_in_dim_reshape.9.mask_ref
  672.4 0.2 broadcast_in_dim.97
  672.6 0.3 broadcast_in_dim_reshape.8.wave_ref
  673.2 12.9 %copy.46 = f32[64,24,1536]{2,0,1:T(8,128)} copy(f32[64,24,1536]{2,1,0:T(8,128)} %bitcast.10) | data formatting | bytes 18874368 | tf_op jit(solution)/shard_map/reshape | solution.py:289
  686.0 189.2 %all-to-all-done.4 = f32[32,48,1536]{2,1,0:T(8,128)} async-done(((f32[32,48,1536]{2,1,0:T(8,128)}), f32[32,48,1536]{2,1,0:T(8,128)}, u32[]{:S(2)}, u32[]{:S(2)}) %all-to-all-start.4) | async-done | bytes 9437216 | tf_op jit(solution)/shard_map/all_to_all | solution.py:266
  875.3 9.3 copy.45
  884.6 3.7 copy-done.1
  888.3 20.6 %shard_map.78.eigen_ref = f32[24,128,1536]{2,1,0:T(8,128)S(1)} custom-call(f32[24,128,1536]{2,1,0:T(8,128)} %q_ref.1, f32[24,1,1536]{2,1,0:T(1,128)S(1)} %broadcast_in_dim_reshape.9.mask_ref, f32[128,128]{1,0:T(8,128)S(1)} %copy-done.4, f32[24,64,1536]{2,1,0:T(8,128)S(1)} %bitcast.52), custom_call_target="tpu_custom_call" | custom-call | flops 3623878656 | bytes 47185920 | tf_op jit(solution)/shard_map/pallas_call | solution.py:147
  908.9 6.8 copy-done
  915.7 26.6 %shard_map.80 = (f32[24,128,1536]{2,1,0:T(8,128)S(1)}, f32[128,128]{1,0:T(8,128)S(1)}, f32[128,128]{1,0:T(8,128)S(1)}) custom-call(f32[24,128,1536]{2,1,0:T(8,128)} %copy-done, f32[24,1,1536]{2,1,0:T(1,128)S(1)} %broadcast_in_dim_reshape.9.mask_ref, f32[24,1,1536]{2,1,0:T(1,128)S(1)} %broadcast_in_dim_reshape.8.wave_ref, f32[128,1]{1,0:T(8,128)S(1)} %copy.37.decay_ref, ...), custom_call_target="tpu_custom_call" | custom-call | tf_op jit(solution)/shard_map/pallas_call | solution.py:202
  942.4 6.8 copy-done.2
  949.5 25.1 %psum.14 = f32[32,32]{0,1:T(8,128)S(1)} all-reduce(f32[32,32]{0,1:T(8,128)S(1)} %slice_add_fusion), channel_id=1, replica_groups=mesh['row'=8,'col'=4] {'row'}, use_global_device_ids=true, to_apply=%region_0.1 | all-reduce | flops 1024 | bytes 8192 | tf_op jit(solution)/shard_map/psum | solution.py:305
  974.6 19.7 %psum.15 = f32[32,32]{0,1:T(8,128)S(1)} all-reduce(f32[32,32]{0,1:T(8,128)S(1)} %psum.14), channel_id=1, replica_groups=mesh['row'=8,'col'=4] {'col'}, use_global_device_ids=true, to_apply=%region_1.2 | all-reduce | flops 1024 | bytes 8192 | tf_op jit(solution)/shard_map/psum | solution.py:305
  994.4 2.9 cholesky.14
  997.4 0.6 compare_reduce_fusion
  998.0 0.7 select_bitcast_fusion
  998.7 2.4 custom-call.7
  1001.1 0.2 fusion.30
  1001.6 0.7 gather_fusion
  1002.3 0.5 log.3
  1002.9 6.4 copy-done.3
  1009.2 16.6 %shard_map.81 = f32[24,128,1536]{2,1,0:T(8,128)} custom-call(f32[24,128,1536]{2,1,0:T(8,128)S(1)} %copy-done.3, f32[128,128]{1,0:T(8,128)S(1)} %mul.191.w_ref), custom_call_target="tpu_custom_call" | custom-call | tf_op jit(solution)/shard_map/pallas_call | solution.py:231
  (44 shorter events, 1.5 us)
Async XLA Ops:
  4.8 22.8 %all-to-all-start.1 = ((f32[32,1,4608]{2,1,0:T(1,128)}), f32[32,1,4608]{2,1,0:T(1,128)S(1)}, u32[]{:S(2)}, u32[]{:S(2)}) async-start(f32[32,1,4608]{2,1,0:T(1,128)} %reshape.171), calls=%async_computation.1 | async-start | bytes 1179648 | tf_op jit(solution)/shard_map/all_to_all | solution.py:266
  12.2 3.7 slice-start
  27.7 0.8 copy-start.6
  28.5 208.2 %all-to-all-start = ((f32[32,48,1536]{2,1,0:T(8,128)}), f32[32,48,1536]{2,1,0:T(8,128)}, u32[]{:S(2)}, u32[]{:S(2)}) async-start(f32[32,48,1536]{2,1,0:T(8,128)} %bitcast.54), calls=%async_computation | async-start | bytes 18874368 | tf_op jit(solution)/shard_map/all_to_all | solution.py:266
  236.7 12.5 %copy-start.7 = (f32[32,1,4608]{2,1,0:T(1,128)S(1)}, f32[32,1,4608]{2,1,0:T(1,128)}, u32[]{:S(2)}) copy-start(f32[32,1,4608]{2,1,0:T(1,128)} %copy-done.6) | copy-start | bytes 1769476
  236.7 212.8 %all-to-all-start.3 = ((f32[32,48,1536]{2,1,0:T(8,128)}), f32[32,48,1536]{2,1,0:T(8,128)}, u32[]{:S(2)}, u32[]{:S(2)}) async-start(f32[32,48,1536]{2,1,0:T(8,128)} %bitcast.53), calls=%async_computation.3 | async-start | bytes 18874368 | tf_op jit(solution)/shard_map/all_to_all | solution.py:266
  449.6 212.8 %all-to-all-start.2 = ((f32[32,48,1536]{2,1,0:T(8,128)}), f32[32,48,1536]{2,1,0:T(8,128)}, u32[]{:S(2)}, u32[]{:S(2)}) async-start(f32[32,48,1536]{2,1,0:T(8,128)} %bitcast.56), calls=%async_computation.2 | async-start | bytes 18874368 | tf_op jit(solution)/shard_map/all_to_all | solution.py:266
  662.4 9.4 copy-start.8
  662.4 10.5 %copy-start.9 = (f32[128]{0:T(128)S(1)}, f32[128]{0:T(128)}, u32[]{:S(2)}) copy-start(f32[128]{0:T(128)} %param.9) | copy-start | bytes 1540
  662.4 10.6 %copy-start.4 = (f32[128,128]{1,0:T(8,128)S(1)}, f32[128,128]{1,0:T(8,128)}, u32[]{:S(2)}) copy-start(f32[128,128]{1,0:T(8,128)} %to_ref.1) | copy-start | bytes 196612
  662.4 212.8 %all-to-all-start.4 = ((f32[32,48,1536]{2,1,0:T(8,128)}), f32[32,48,1536]{2,1,0:T(8,128)}, u32[]{:S(2)}, u32[]{:S(2)}) async-start(f32[32,48,1536]{2,1,0:T(8,128)} %bitcast.55), calls=%async_computation.4 | async-start | bytes 18874368 | tf_op jit(solution)/shard_map/all_to_all | solution.py:266
  884.6 3.7 copy-start.1
  888.3 27.4 %copy-start.5 = (f32[128,128]{1,0:T(8,128)S(1)}, f32[128,128]{1,0:T(8,128)}, u32[]{:S(2)}) copy-start(f32[128,128]{1,0:T(8,128)} %from_ref.1) | copy-start | bytes 196612
  908.9 6.9 copy-start
  942.4 6.9 copy-start.2
  1002.9 6.4 copy-start.3
